TPU v7x, 8 devices: a whole 2x2x1 slice. The times are simulated.
8 devices in a mesh: pod: 2 (over z, y), data: 4 (over x, core).
Axes of the slice: x: 2, y: 2, z: 1, core: 2. Of those that a mesh axis runs over, the one named last changes fastest.
Arguments:
- feat_a: bfloat16 [8192, 2048], P(('pod', 'data'))
- feat_b: bfloat16 [8192, 2048], P(('pod', 'data'))
- w_first: bfloat16 [2048, 2048], replicated
- w_second: bfloat16 [2048, 2048], replicated
- w_third: bfloat16 [2048, 2048], replicated
- gain_first: float32 [2048], replicated
- shift_first: float32 [2048], replicated
- gain_second: float32 [2048], replicated
- shift_second: float32 [2048], replicated
- lam_off: float32 [], replicated
Outputs:
- output 1: float32 [], replicated
- output 2: float32 [2048, 2048], replicated
- output 3: float32 [2048, 2048], replicated
- output 4: float32 [2048, 2048], replicated
- output 5: float32 [2048], replicated
- output 6: float32 [2048], replicated
- output 7: float32 [2048], replicated
- output 8: float32 [2048], replicated
All inputs are finite; a program needn't handle non-finite values.
Results may differ from a plain program's by a relative error of at most 0.001.
Values are sent between devices in bfloat16 or wider.
A program may use at most 1 GiB of HBM per device.

v0:
```python
import functools
import jax
import jax.numpy as jnp
from jax import lax
from jax.sharding import PartitionSpec as P, NamedSharding

BN_EPS = 1e-5
ROW_AXES = ('pod', 'data')


def batch_norm(pre_act, num_rows):
    local_sums = jnp.stack([jnp.sum(pre_act, axis=1), jnp.sum(pre_act * pre_act, axis=1)])
    totals = lax.psum(local_sums, ROW_AXES) / num_rows
    inv_std = lax.rsqrt(totals[1] - totals[0] * totals[0] + BN_EPS)[:, None, :]
    return (pre_act - totals[0][:, None, :]) * inv_std, inv_std


def run_layer(hidden, weight, gain_vec, shift_vec, num_rows):
    pre_act = jnp.einsum('vnf,fd->vnd', hidden, weight, preferred_element_type=jnp.float32)
    normed, inv_std = batch_norm(pre_act, num_rows)
    post_affine = gain_vec * normed + shift_vec
    return jnp.maximum(post_affine, 0.0).astype(jnp.bfloat16), post_affine, normed, inv_std


def norm_backward(grad_norm, normed, inv_std, num_rows):
    local_sums = jnp.stack([jnp.sum(grad_norm, axis=1), jnp.sum(grad_norm * normed, axis=1)])
    totals = lax.psum(local_sums, ROW_AXES) / num_rows
    return inv_std * (grad_norm - totals[0][:, None, :] - normed * totals[1][:, None, :])


def affine_backward(grad_hid, post_affine, normed, inv_std, gain_vec, num_rows):
    grad_act = jnp.where(post_affine > 0, grad_hid, 0.0)
    local_sums = jnp.stack([jnp.sum(grad_act * normed, axis=1), jnp.sum(grad_act, axis=1)])
    totals = lax.psum(local_sums, ROW_AXES)
    grad_pre = (gain_vec * inv_std) * (grad_act - totals[1][:, None, :] / num_rows - normed * (totals[0][:, None, :] / num_rows))
    return grad_pre.astype(jnp.bfloat16), jnp.sum(totals[0], axis=0), jnp.sum(totals[1], axis=0)


def loss_and_grad(corr_mat, lam_off):
    on_diag = jnp.diagonal(corr_mat)
    total_loss = jnp.sum((1.0 - on_diag) ** 2) + lam_off * (jnp.sum(corr_mat * corr_mat) - jnp.sum(on_diag * on_diag))
    diag_mask = lax.broadcasted_iota(jnp.int32, corr_mat.shape, 0) == lax.broadcasted_iota(jnp.int32, corr_mat.shape, 1)
    grad_corr = jnp.where(diag_mask, -2.0 * (1.0 - corr_mat), 2.0 * lam_off * corr_mat)
    return total_loss, grad_corr.astype(jnp.bfloat16)


def device_step(num_dev, feat_a, feat_b, w_first, w_second, w_third, gain_first, shift_first, gain_second, shift_second, lam_off):
    num_rows = feat_a.shape[0] * num_dev
    both_views = jnp.stack([feat_a, feat_b])
    hid_one, post_one, norm_one, inv_one = run_layer(both_views, w_first, gain_first, shift_first, num_rows)
    hid_two, post_two, norm_two, inv_two = run_layer(hid_one, w_second, gain_second, shift_second, num_rows)
    proj_out = jnp.einsum('vnf,fd->vnd', hid_two, w_third, preferred_element_type=jnp.float32)
    emb_norm, inv_three = batch_norm(proj_out, num_rows)
    emb_bf = emb_norm.astype(jnp.bfloat16)
    corr_part = lax.dot_general(emb_bf[0], emb_bf[1], (((0,), (0,)), ((), ())), preferred_element_type=jnp.float32)
    corr_mat = lax.psum(corr_part, ROW_AXES) / num_rows
    total_loss, grad_corr = loss_and_grad(corr_mat, lam_off)
    grad_emb_a = lax.dot_general(emb_bf[1], grad_corr, (((1,), (1,)), ((), ())), preferred_element_type=jnp.float32)
    grad_emb_b = jnp.dot(emb_bf[0], grad_corr, preferred_element_type=jnp.float32)
    grad_emb = jnp.stack([grad_emb_a, grad_emb_b]) / num_rows
    grad_proj = norm_backward(grad_emb, emb_norm, inv_three, num_rows).astype(jnp.bfloat16)
    grad_third = lax.psum(jnp.einsum('woe,wof->ef', hid_two, grad_proj, preferred_element_type=jnp.float32), ROW_AXES)
    grad_hid_two = jnp.einsum('wof,ef->woe', grad_proj, w_third, preferred_element_type=jnp.float32)
    grad_pre_two, grad_gain_second, grad_shift_second = affine_backward(grad_hid_two, post_two, norm_two, inv_two, gain_second, num_rows)
    grad_second = lax.psum(jnp.einsum('woe,wof->ef', hid_one, grad_pre_two, preferred_element_type=jnp.float32), ROW_AXES)
    grad_hid_one = jnp.einsum('wof,ef->woe', grad_pre_two, w_second, preferred_element_type=jnp.float32)
    grad_pre_one, grad_gain_first, grad_shift_first = affine_backward(grad_hid_one, post_one, norm_one, inv_one, gain_first, num_rows)
    grad_first = lax.psum(jnp.einsum('vnf,vnd->fd', both_views, grad_pre_one, preferred_element_type=jnp.float32), ROW_AXES)
    return (total_loss, grad_first, grad_second, grad_third, grad_gain_first, grad_shift_first, grad_gain_second, grad_shift_second)


def solution(mesh):
    num_dev = mesh.shape['pod'] * mesh.shape['data']
    row_spec = P(ROW_AXES, None)
    repl_spec = P()
    return jax.shard_map(functools.partial(device_step, num_dev), mesh=mesh, in_specs=(row_spec, row_spec, repl_spec, repl_spec, repl_spec, repl_spec, repl_spec, repl_spec, repl_spec, repl_spec), out_specs=(repl_spec, repl_spec, repl_spec, repl_spec, repl_spec, repl_spec, repl_spec, repl_spec), check_vma=False)
```

profile of v0, /device:TPU:0, one launch (start us, length us, event | category | flops | bytes accessed | tf_op | source)
XLA Modules:
  0.0 1275.8 jit_solution(9373283312920070233)
XLA Ops:
  7.2 0.0 all-reduce.4.cloned.1.call-start
  7.2 0.0 copy-start.9
  7.2 0.0 copy-start.12
  7.2 24.2 %fusion.37 = (f32[2,2048]{1,0:T(2,128)S(1)}, f32[2,2048]{1,0:T(2,128)S(1)}, f32[2,1024,2048]{2,1,0:T(8,128)}) fusion(bf16[2048,2048]{1,0:T(8,128)(2,1)} %param.12, bf16[1,1024,2048]{2,1,0:T(8,128)(2,1)} %bitcast.135, bf16[1,1024,2048]{2,1,0:T(8,128)(2,1)} %bitcast.137), kind=kOutput, calls=%fused_computation.94 | convolution fusion | flops 17196638208 | bytes 33587200 | tf_op jit(solution)/shard_map/vnf,fd->vnd/dot_general | solution.py:19
  31.5 25.2 %psum.70 = f32[2,2,2048]{2,1,0:T(2,128)S(1)} all-reduce(f32[2,2,2048]{2,1,0:T(2,128)S(1)} %pad_maximum_fusion.3), channel_id=1, replica_groups=mesh['pod'=2,'data'=4] {'pod','data'}, use_global_device_ids=true, to_apply=%region_2.0 | all-reduce | flops 8192 | bytes 65536 | tf_op jit(solution)/shard_map/psum | solution.py:13
  56.8 0.6 fusion.32
  57.4 0.0 copy-done.12
  57.4 24.9 %fusion.36 = (f32[2,2048]{1,0:T(2,128)S(1)}, f32[2,2048]{1,0:T(2,128)S(1)}, f32[2,1024,2048]{2,1,0:T(8,128)}) fusion(bf16[2048,2048]{1,0:T(8,128)(2,1)} %param.13, f32[2,1024,2048]{2,1,0:T(8,128)} %get-tuple-element.41, f32[2048]{0:T(1024)S(1)} %copy-done.12, f32[2,2048]{1,0:T(2,128)S(1)} %get-tuple-element.36, f32[2,2048]{1,0:T(2,128)S(1)} %slice_bitcast_fusion.13, ...), kind=kOutput, calls=%fused_computation.93 | convolution fusion | flops 17217609728 | bytes 42024960 | tf_op jit(solution)/shard_map/vnf,fd->vnd/dot_general | solution.py:19
  82.4 23.2 %psum.71 = f32[2,2,2048]{2,1,0:T(2,128)S(1)} all-reduce(f32[2,2,2048]{2,1,0:T(2,128)S(1)} %pad_maximum_fusion.4), channel_id=1, replica_groups=mesh['pod'=2,'data'=4] {'pod','data'}, use_global_device_ids=true, to_apply=%region_5.0 | all-reduce | flops 8192 | bytes 65536 | tf_op jit(solution)/shard_map/psum | solution.py:13
  105.6 0.6 fusion.28
  106.2 0.0 copy-done.14
  106.2 24.9 %fusion.35 = (f32[2,2048]{1,0:T(2,128)S(1)}, f32[2,2048]{1,0:T(2,128)S(1)}, f32[2,1024,2048]{2,1,0:T(8,128)}) fusion(bf16[2048,2048]{1,0:T(8,128)(2,1)} %param.14, f32[2,1024,2048]{2,1,0:T(8,128)} %get-tuple-element.42, f32[2048]{0:T(1024)S(1)} %copy-done.14, f32[2,2048]{1,0:T(2,128)S(1)} %get-tuple-element.38, f32[2,2048]{1,0:T(2,128)S(1)} %slice_bitcast_fusion.11, ...), kind=kOutput, calls=%fused_computation.92 | convolution fusion | flops 17217609728 | bytes 42024960 | tf_op jit(solution)/shard_map/vnf,fd->vnd/dot_general | solution.py:52
  131.1 24.6 %psum.72 = f32[2,2,2048]{2,1,0:T(2,128)S(1)} all-reduce(f32[2,2,2048]{2,1,0:T(2,128)S(1)} %pad_maximum_fusion.5), channel_id=1, replica_groups=mesh['pod'=2,'data'=4] {'pod','data'}, use_global_device_ids=true, to_apply=%region_8.0 | all-reduce | flops 8192 | bytes 65536 | tf_op jit(solution)/shard_map/psum | solution.py:13
  155.8 7.3 fusion
  163.0 3.2 copy-done.2
  166.2 11.5 fusion.21
  177.7 0.0 all-reduce.4.cloned.1.call-update
  177.8 0.0 all-reduce.6.cloned.1.call-start
  178.5 206.5 %all-reduce.4.cloned.1.call-done = f32[2048,2048]{1,0:T(8,128)} async-done(((f32[2048,2048]{1,0:T(8,128)}), f32[2048,2048]{1,0:T(8,128)}) %all-reduce.4.cloned.1.call-update) | async-done | bytes 16777232 | tf_op jit(solution)/shard_map/psum | solution.py:56
  385.0 13.2 %convolution_bitcast_fusion.3 = f32[1,1024,2048]{2,1,0:T(8,128)S(1)} fusion(bf16[2,1024,2048]{2,1,0:T(8,128)(2,1)} %copy-done.2, f32[2048,2048]{1,0:T(8,128)} %all-reduce.4.cloned.1.call-done, f32[]{:T(128)S(6)} %mul.209), kind=kOutput, calls=%fused_computation.45 | convolution fusion | flops 8619294720 | bytes 29360132 | tf_op jit(solution)/shard_map/dot_general | solution.py:59
  398.2 18.7 %convolution_bitcast_fusion.4 = f32[1,1024,2048]{2,1,0:T(8,128)} fusion(bf16[2,1024,2048]{2,1,0:T(8,128)(2,1)} %copy-done.2, f32[2048,2048]{1,0:T(8,128)} %all-reduce.4.cloned.1.call-done, f32[]{:T(128)S(6)} %mul.209), kind=kOutput, calls=%fused_computation.46 | convolution fusion | flops 8619294720 | bytes 29360132 | tf_op jit(solution)/shard_map/dot_general | solution.py:58
  417.0 10.0 fusion.1
  427.0 22.5 %psum.74 = f32[2,2,2048]{2,1,0:T(2,128)S(1)} all-reduce(f32[2,2,2048]{2,1,0:T(2,128)S(1)} %pad_maximum_fusion.6), channel_id=1, replica_groups=mesh['pod'=2,'data'=4] {'pod','data'}, use_global_device_ids=true, to_apply=%region_15.16 | all-reduce | flops 8192 | bytes 65536 | tf_op jit(solution)/shard_map/psum | solution.py:27
  449.6 15.3 %multiply_convert_fusion.2 = bf16[2,1024,2048]{2,1,0:T(8,128)(2,1)} fusion(f32[2,1024,2048]{2,1,0:T(8,128)} %get-tuple-element.43, f32[1,1024,2048]{2,1,0:T(8,128)} %copy-done, f32[1,1024,2048]{2,1,0:T(8,128)} %convolution_bitcast_fusion.4, f32[2,2048]{1,0:T(2,128)S(1)} %get-tuple-element.40, f32[2,2048]{1,0:T(2,128)S(1)} %get-tuple-element.39, ...), kind=kLoop, calls=%fused_computation.6 | loop fusion | flops 37748736 | bytes 42008576 | tf_op jit(solution)/shard_map/convert_element_type | solution.py:61
  464.9 28.8 %multiply_reduce_fusion.1 = (f32[2,2048]{1,0:T(2,128)S(1)}, f32[2,2048]{1,0:T(2,128)S(1)}, f32[2,1024,2048]{2,1,0:T(8,128)}) fusion(f32[2,1024,2048]{2,1,0:T(8,128)} %get-tuple-element.42, f32[2,2048]{1,0:T(2,128)S(1)} %get-tuple-element.38, f32[2,2048]{1,0:T(2,128)S(1)} %slice_bitcast_fusion.11, bf16[2,1024,2048]{2,1,0:T(8,128)(2,1)} %multiply_convert_fusion.2, ...), kind=kOutput, calls=%fused_computation.5 | convolution fusion | flops 17217609728 | bytes 50413568 | tf_op jit(solution)/shard_map/wof,ef->woe/dot_general | solution.py:63
  493.8 24.3 %psum.75 = f32[2,2,2048]{2,1,0:T(2,128)S(1)} all-reduce(f32[2,2,2048]{2,1,0:T(2,128)S(1)} %pad_maximum_fusion.7), channel_id=1, replica_groups=mesh['pod'=2,'data'=4] {'pod','data'}, use_global_device_ids=true, to_apply=%region_18.19 | all-reduce | flops 8192 | bytes 65536 | tf_op jit(solution)/shard_map/psum | solution.py:34
  518.1 0.6 slice_reduce_fusion.3
  518.8 0.0 copy-start.13
  518.8 15.2 %multiply_convert_fusion.1 = bf16[2,1024,2048]{2,1,0:T(8,128)(2,1)} fusion(f32[2,1024,2048]{2,1,0:T(8,128)} %get-tuple-element.44, f32[2,1024,2048]{2,1,0:T(8,128)} %get-tuple-element.42, f32[2,2048]{1,0:T(2,128)S(1)} %get-tuple-element.31, f32[2,2048]{1,0:T(2,128)S(1)} %get-tuple-element.32, f32[2,2048]{1,0:T(2,128)S(1)} %copy-done.3, ...), kind=kLoop, calls=%fused_computation.4 | loop fusion | flops 29360128 | bytes 42024960 | tf_op jit(solution)/shard_map/convert_element_type | solution.py:36
  534.0 0.0 copy-done.5
  534.0 28.9 %multiply_reduce_fusion = (f32[2,2048]{1,0:T(2,128)S(1)}, f32[2,2048]{1,0:T(2,128)S(1)}, f32[2,1024,2048]{2,1,0:T(8,128)}) fusion(f32[2,1024,2048]{2,1,0:T(8,128)} %get-tuple-element.41, f32[2,2048]{1,0:T(2,128)S(1)} %copy-done.8, f32[2,2048]{1,0:T(2,128)S(1)} %copy-done.5, bf16[2,1024,2048]{2,1,0:T(8,128)(2,1)} %multiply_convert_fusion.1, ...), kind=kOutput, calls=%fused_computation.3 | convolution fusion | flops 17217609728 | bytes 50413568 | tf_op jit(solution)/shard_map/wof,ef->woe/dot_general | solution.py:66
  562.9 25.3 %convolution_bitcast_fusion.1 = f32[2048,2048]{1,0:T(8,128)} fusion(bf16[2,1024,2048]{2,1,0:T(8,128)(2,1)} %multiply_convert_fusion.1, f32[2,1024,2048]{2,1,0:T(8,128)} %get-tuple-element.41, f32[2048]{0:T(1024)S(1)} %copy-done.13, f32[2,2048]{1,0:T(2,128)S(1)} %copy-done.8, f32[2,2048]{1,0:T(2,128)S(1)} %copy-done.5, f32[2048]{0:T(1024)S(1)} %copy-done.10), kind=kOutput, calls=%fused_computation.26 | convolution fusion | flops 17205035008 | bytes 41992192 | tf_op jit(solution)/shard_map/woe,wof->ef/dot_general | solution.py:65
  588.2 25.5 %convolution_bitcast_fusion = f32[2048,2048]{1,0:T(8,128)} fusion(bf16[2,1024,2048]{2,1,0:T(8,128)(2,1)} %multiply_convert_fusion.2, f32[2,1024,2048]{2,1,0:T(8,128)} %get-tuple-element.42, f32[2048]{0:T(1024)S(1)} %copy-done.14, f32[2,2048]{1,0:T(2,128)S(1)} %get-tuple-element.38, f32[2,2048]{1,0:T(2,128)S(1)} %slice_bitcast_fusion.11, f32[2048]{0:T(1024)S(1)} %copy-done.11), kind=kOutput, calls=%fused_computation.25 | convolution fusion | flops 17205035008 | bytes 41992192 | tf_op jit(solution)/shard_map/woe,wof->ef/dot_general | solution.py:62
  613.7 23.2 %psum.76 = f32[2,2,2048]{2,1,0:T(2,128)S(1)} all-reduce(f32[2,2,2048]{2,1,0:T(2,128)S(1)} %pad_maximum_fusion.8), channel_id=1, replica_groups=mesh['pod'=2,'data'=4] {'pod','data'}, use_global_device_ids=true, to_apply=%region_21.22 | all-reduce | flops 8192 | bytes 65536 | tf_op jit(solution)/shard_map/psum | solution.py:34
  636.9 0.6 slice_reduce_fusion.1
  637.6 27.1 %convolution_bitcast_fusion.2 = f32[2048,2048]{1,0:T(8,128)} fusion(f32[2,1024,2048]{2,1,0:T(8,128)} %get-tuple-element.45, f32[2,1024,2048]{2,1,0:T(8,128)} %get-tuple-element.41, f32[2,2048]{1,0:T(2,128)S(1)} %get-tuple-element.33, f32[2,2048]{1,0:T(2,128)S(1)} %get-tuple-element.34, f32[2,2048]{1,0:T(2,128)S(1)} %copy-done.6, ...), kind=kOutput, calls=%fused_computation.27 | convolution fusion | flops 17213423616 | bytes 58802176 | tf_op jit(solution)/shard_map/vnf,vnd->fd/dot_general | solution.py:68
  664.7 0.0 all-reduce.6.cloned.1.call-update
  664.7 13.5 %multiply_reduce_fusion.3 = (f32[]{:T(128)}, f32[2048,2048]{1,0:T(8,128)}) fusion(f32[2048,2048]{1,0:T(8,128)} %all-reduce.4.cloned.1.call-done), kind=kLoop, calls=%fused_computation.10 | loop fusion | flops 12582911 | bytes 33554436 | tf_op jit(solution)/shard_map/reduce_sum | solution.py:41
  678.2 33.8 %gather_fusion = f32[2048]{0:T(1024)S(1)} fusion(f32[2048,2048]{1,0:T(8,128)} %get-tuple-element.30, s32[2048]{0:T(1024)S(1)} %bitcast.120), kind=kCustom, calls=%fused_computation | custom fusion | bytes 32768 | tf_op jit(solution)/shard_map/jit(diagonal)/cond/branch_0_fun/gather | solution.py:40
  712.0 0.6 multiply_reduce_fusion.7
  714.6 519.2 %all-reduce.6.cloned.1.call-done = (f32[2048,2048]{1,0:T(8,128)}, f32[2048,2048]{1,0:T(8,128)}, f32[2048,2048]{1,0:T(8,128)}) async-done(((f32[2048,2048]{1,0:T(8,128)}, f32[2048,2048]{1,0:T(8,128)}, f32[2048,2048]{1,0:T(8,128)}), (f32[2048,2048]{1,0:T(8,128)}, f32[2048,2048]{1,0:T(8,128)}, f32[2048,2048]{1,0:T(8,128)})) %all-reduce.6.cloned.1.call-update) | async-done | bytes 50331664 | tf_op jit(solution)/shard_map/psum | solution.py:68
  1233.7 13.5 %copy.32 = f32[2048,2048]{1,0:T(8,128)} copy(f32[2048,2048]{1,0:T(8,128)} %get-tuple-element.47) | data formatting | bytes 33554432
  1247.3 2.9 copy-done.1
  1250.2 8.5 copy.33
  1258.7 0.0 slice-done
  1258.7 1.4 slice-done.2
  1260.1 1.2 slice-done.3
  1261.2 6.2 copy.34
  (44 shorter events, 0.3 us)
Async XLA Ops:
  7.2 377.8 %all-reduce.4.cloned.1.call-start = ((), (), s32[]{:S(2)}) async-start(), calls=%async_computation | async-start | bytes 33554432 | tf_op jit(solution)/shard_map/psum | solution.py:56
  7.2 49.6 %copy-start.9 = (f32[2048]{0:T(1024)S(1)}, f32[2048]{0:T(1024)}, u32[]{:S(2)}) copy-start(f32[2048]{0:T(1024)} %param.15) | copy-start | bytes 24580
  7.2 50.2 %copy-start.12 = (f32[2048]{0:T(1024)S(1)}, f32[2048]{0:T(1024)}, u32[]{:S(2)}) copy-start(f32[2048]{0:T(1024)} %param.16) | copy-start | bytes 24580
  56.8 25.5 %copy-start.4 = (f32[2,2048]{1,0:T(2,128)}, f32[2,2048]{1,0:T(2,128)S(1)}, u32[]{:S(2)}) copy-start(f32[2,2048]{1,0:T(2,128)S(1)} %slice_bitcast_fusion.13) | copy-start | bytes 49156
  57.4 24.9 %copy-start.7 = (f32[2,2048]{1,0:T(2,128)}, f32[2,2048]{1,0:T(2,128)S(1)}, u32[]{:S(2)}) copy-start(f32[2,2048]{1,0:T(2,128)S(1)} %get-tuple-element.36) | copy-start | bytes 49156
  57.4 48.2 %copy-start.11 = (f32[2048]{0:T(1024)S(1)}, f32[2048]{0:T(1024)}, u32[]{:S(2)}) copy-start(f32[2048]{0:T(1024)} %param.17) | copy-start | bytes 24580
  57.4 48.8 %copy-start.14 = (f32[2048]{0:T(1024)S(1)}, f32[2048]{0:T(1024)}, u32[]{:S(2)}) copy-start(f32[2048]{0:T(1024)} %param.18) | copy-start | bytes 24580
  163.0 3.2 copy-start.2
  177.8 1056.0 %all-reduce.6.cloned.1.call-start = ((), (), s32[]{:S(2)}) async-start(), calls=%async_computation.1 | async-start | bytes 100663296 | tf_op jit(solution)/shard_map/psum | solution.py:68
  398.2 18.8 %copy-start = (f32[1,1024,2048]{2,1,0:T(8,128)}, f32[1,1024,2048]{2,1,0:T(8,128)S(1)}, u32[]{:S(2)}) copy-start(f32[1,1024,2048]{2,1,0:T(8,128)S(1)} %convolution_bitcast_fusion.3) | copy-start | bytes 25165828
  464.9 53.9 %copy-start.3 = (f32[2,2048]{1,0:T(2,128)S(1)}, f32[2,2048]{1,0:T(2,128)}, u32[]{:S(2)}) copy-start(f32[2,2048]{1,0:T(2,128)} %get-tuple-element.37) | copy-start | bytes 49156
  518.8 15.2 %copy-start.5 = (f32[2,2048]{1,0:T(2,128)S(1)}, f32[2,2048]{1,0:T(2,128)}, u32[]{:S(2)}) copy-start(f32[2,2048]{1,0:T(2,128)} %copy-done.4) | copy-start | bytes 49156
  518.8 15.2 %copy-start.8 = (f32[2,2048]{1,0:T(2,128)S(1)}, f32[2,2048]{1,0:T(2,128)}, u32[]{:S(2)}) copy-start(f32[2,2048]{1,0:T(2,128)} %copy-done.7) | copy-start | bytes 49156
  518.8 15.2 %copy-start.10 = (f32[2048]{0:T(1024)S(1)}, f32[2048]{0:T(1024)}, u32[]{:S(2)}) copy-start(f32[2048]{0:T(1024)} %param.15) | copy-start | bytes 24580
  518.8 15.2 %copy-start.13 = (f32[2048]{0:T(1024)S(1)}, f32[2048]{0:T(1024)}, u32[]{:S(2)}) copy-start(f32[2048]{0:T(1024)} %param.16) | copy-start | bytes 24580
  588.2 49.4 %copy-start.6 = (f32[2,2048]{1,0:T(2,128)S(1)}, f32[2,2048]{1,0:T(2,128)}, u32[]{:S(2)}) copy-start(f32[2,2048]{1,0:T(2,128)} %get-tuple-element.35) | copy-start | bytes 49156
  1233.7 16.4 %copy-start.1 = (f32[2048,2048]{1,0:T(8,128)S(1)}, f32[2048,2048]{1,0:T(8,128)}, u32[]{:S(2)}) copy-start(f32[2048,2048]{1,0:T(8,128)} %get-tuple-element.48) | copy-start | bytes 50331652
  1233.7 24.9 %slice-start = ((s8[16777216]{0:T(1024)(128)(4,1)}), s8[4194304]{0:T(1024)(128)(4,1)S(1)}, s32[]{:S(2)}) async-start(s8[16777216]{0:T(1024)(128)(4,1)} %bitcast.121), calls=%async_computation.2 | async-start | bytes 8388608
  1233.7 24.9 %slice-start.1 = ((s8[16777216]{0:T(1024)(128)(4,1)}), s8[4194304]{0:T(1024)(128)(4,1)S(1)}, s32[]{:S(2)}) async-start(s8[16777216]{0:T(1024)(128)(4,1)} %bitcast.121), calls=%async_computation.3 | async-start | bytes 8388608
  1250.2 9.9 slice-start.2
  1250.2 11.1 slice-start.3
Sparse Core Ops, SparseCore 0:
  177.9 207.0 all-reduce.3
  664.8 568.8 all-reduce.5
where the time goes:
time: 1290 us; the launch traced here: 1280 us
  waiting for transfers between devices  726 us (56%)
  matrix products  253 us (20%)
  blocking collectives  143 us (11%)
  local copies, waits for them, and re-layouts  70.8 us (5%)
  other arithmetic  64.6 us (5%)
  between operations  18.5 us (1%)
    psum x1, waiting for transfers between devices, device_step(): lax.psum(jnp.einsum('vnf,vnd->fd', both_views, grad_pre_one, preferred_el...  519 us
    psum x1, waiting for transfers between devices, device_step(): corr_mat = lax.psum(corr_part, ROW_AXES) / num_rows  206 us
    psum x3, blocking collectives, batch_norm(): totals = lax.psum(local_sums, ROW_AXES) / num_rows  73 us
    dot_general x2, matrix products, run_layer(): jnp.einsum('vnf,fd->vnd', hidden, weight, preferred_element_type=jnp.floa...  49.1 us
    psum x2, blocking collectives, affine_backward(): totals = lax.psum(local_sums, ROW_AXES)  47.5 us
    unnamed x41, local copies, waits for them, and re-layouts  36.9 us
    gather x1, local copies, waits for them, and re-layouts, loss_and_grad(): on_diag = jnp.diagonal(corr_mat)  33.8 us
    dot_general x1, matrix products, device_step(): jnp.einsum('wof,ef->woe', grad_pre_two, w_second, preferred_element_type=...  28.9 us
  transfers between devices with their start and end apart: 2, of which 2 were waited for; matrix products, arithmetic and copies ran while one was open for 4% of the time, Pallas kernels for 0%

commit v1 on v0

v1 whole, which is shorter than its diff:
```python
import functools
import jax
import jax.numpy as jnp
from jax import lax
from jax.experimental import pallas as pl
from jax.experimental.pallas import tpu as pltpu
from jax.sharding import PartitionSpec as P

BN_EPS = 1e-5
ROW_AXES = ('pod', 'data')
NDEV = 8
BLK = 256


def exchange_kernel(in_ref, out_ref, slots, send_sems, recv_sems):
    pod = lax.axis_index('pod')
    data = lax.axis_index('data')
    me = pod * 4 + data
    barrier = pltpu.get_barrier_semaphore()
    for off in range(1, NDEV):
        peer = lax.rem(me + off, NDEV)
        pl.semaphore_signal(barrier, inc=1, device_id=(peer // 4, lax.rem(peer, 4)), device_id_type=pl.DeviceIdType.MESH)
    pl.semaphore_wait(barrier, NDEV - 1)
    copies = []
    for off in range(1, NDEV):
        peer = lax.rem(me + off, NDEV)
        copy = pltpu.make_async_remote_copy(
            src_ref=in_ref, dst_ref=slots.at[off], send_sem=send_sems.at[off], recv_sem=recv_sems.at[off],
            device_id=(peer // 4, lax.rem(peer, 4)), device_id_type=pl.DeviceIdType.MESH)
        copy.start()
        copies.append(copy)
    slots[0] = in_ref[...]
    for copy in copies:
        copy.wait()
    total = slots[me]
    for src in range(1, NDEV):
        total = total + slots[lax.rem(me + NDEV - src, NDEV)]
    out_ref[...] = total


def sum_devices(vals, cid):
    return pl.pallas_call(
        exchange_kernel,
        out_shape=jax.ShapeDtypeStruct(vals.shape, vals.dtype),
        in_specs=[pl.BlockSpec(memory_space=pltpu.VMEM)],
        out_specs=pl.BlockSpec(memory_space=pltpu.VMEM),
        scratch_shapes=[pltpu.VMEM((NDEV,) + vals.shape, vals.dtype), pltpu.SemaphoreType.DMA((NDEV,)), pltpu.SemaphoreType.DMA((NDEV,))],
        compiler_params=pltpu.CompilerParams(collective_id=cid, has_side_effects=True),
        name='stat_sum',
    )(vals)


CORE_PERM = [(d, d ^ 1) for d in range(8)]
FIRST_PERM = [(d, d ^ 2 if d % 2 == 0 else d ^ 4) for d in range(8)]
SECOND_PERM = [(d, d ^ 4 if d % 2 == 0 else d ^ 2) for d in range(8)]


def send(block, perm):
    return lax.ppermute(block, ROW_AXES, perm)


def place():
    y = lax.axis_index('pod')
    xc = lax.axis_index('data')
    core, x = lax.rem(xc, 2), xc // 2
    key1 = jnp.where(core == 0, x, y)
    key2 = jnp.where(core == 0, y, x)
    return core, key1, key2


def block_of(mat, idx):
    return lax.dynamic_slice_in_dim(mat, idx * BLK, BLK, axis=0)


def reduce_block(theirs, ours, where):
    core, key1, key2 = where
    got = send(theirs, CORE_PERM)
    b_sf, b_sk = (1 - key1) * 2 + 1 - key2, (1 - key1) * 2 + key2
    b_kf, b_kk = key1 * 2 + 1 - key2, key1 * 2 + key2
    in_f = send(block_of(ours, b_sf) + block_of(got, b_sf), FIRST_PERM)
    in_k = send(block_of(ours, b_sk) + block_of(got, b_sk), FIRST_PERM)
    in_2 = send(block_of(ours, b_kf) + block_of(got, b_kf) + in_f, SECOND_PERM)
    return block_of(ours, b_kk) + block_of(got, b_kk) + in_k + in_2


def gather_blocks(fin, where):
    core, key1, key2 = where
    a = send(fin, SECOND_PERM)
    b = send(fin, FIRST_PERM)
    c = send(a, FIRST_PERM)
    out = jnp.zeros((8 * BLK, fin.shape[1]), fin.dtype)
    mine = [(fin, key1 * 2 + key2), (a, key1 * 2 + 1 - key2), (b, (1 - key1) * 2 + key2), (c, (1 - key1) * 2 + 1 - key2)]
    other = [(fin, key2 * 2 + key1), (a, key2 * 2 + 1 - key1), (b, (1 - key2) * 2 + key1), (c, (1 - key2) * 2 + 1 - key1)]
    for (blk, idx), (_, oidx) in zip(mine, other):
        far = send(blk, CORE_PERM)
        out = lax.dynamic_update_slice_in_dim(out, blk, (core * 4 + idx) * BLK, axis=0)
        out = lax.dynamic_update_slice_in_dim(out, far, ((1 - core) * 4 + oidx) * BLK, axis=0)
    return out


def dot_rows(lhs, rhs):
    return lax.dot_general(lhs, rhs, (((0,), (0,)), ((), ())), preferred_element_type=jnp.float32)


def weight_grad(lhs, rhs, where):
    core = where[0]
    theirs = dot_rows(lax.dynamic_slice_in_dim(lhs, (1 - core) * 1024, 1024, axis=1), rhs)
    ours = dot_rows(lax.dynamic_slice_in_dim(lhs, core * 1024, 1024, axis=1), rhs)
    return reduce_block(theirs, ours, where)


def stats(pre_act):
    return jnp.stack([jnp.sum(pre_act, axis=1), jnp.sum(pre_act * pre_act, axis=1)])


def batch_norm(pre_act, num_rows, cid):
    totals = sum_devices(stats(pre_act).reshape(4, -1), cid).reshape(2, 2, -1) / num_rows
    inv_std = lax.rsqrt(totals[1] - totals[0] * totals[0] + BN_EPS)[:, None, :]
    return (pre_act - totals[0][:, None, :]) * inv_std, inv_std


def run_layer(hidden, weight, gain_vec, shift_vec, num_rows, cid):
    pre_act = jnp.einsum('vnf,fd->vnd', hidden, weight, preferred_element_type=jnp.float32)
    normed, inv_std = batch_norm(pre_act, num_rows, cid)
    post_affine = gain_vec * normed + shift_vec
    return jnp.maximum(post_affine, 0.0).astype(jnp.bfloat16), post_affine, normed, inv_std


def affine_backward(grad_hid, post_affine, normed, inv_std, gain_vec, num_rows, cid):
    grad_act = jnp.where(post_affine > 0, grad_hid, 0.0)
    local_sums = jnp.stack([jnp.sum(grad_act * normed, axis=1), jnp.sum(grad_act, axis=1)])
    totals = sum_devices(local_sums.reshape(4, -1), cid).reshape(2, 2, -1)
    grad_pre = (gain_vec * inv_std) * (grad_act - totals[1][:, None, :] / num_rows - normed * (totals[0][:, None, :] / num_rows))
    return grad_pre.astype(jnp.bfloat16), jnp.sum(totals[0], axis=0), jnp.sum(totals[1], axis=0)


def device_step(feat_a, feat_b, w_first, w_second, w_third, gain_first, shift_first, gain_second, shift_second, lam_off):
    num_rows = feat_a.shape[0] * NDEV
    where = place()
    core, key1, key2 = where
    both_views = jnp.stack([feat_a, feat_b])
    hid_one, post_one, norm_one, inv_one = run_layer(both_views, w_first, gain_first, shift_first, num_rows, 0)
    hid_two, post_two, norm_two, inv_two = run_layer(hid_one, w_second, gain_second, shift_second, num_rows, 1)
    proj_out = jnp.einsum('vnf,fd->vnd', hid_two, w_third, preferred_element_type=jnp.float32)
    emb_norm, inv_three = batch_norm(proj_out, num_rows, 2)
    emb_bf = emb_norm.astype(jnp.bfloat16)
    corr_blk = weight_grad(emb_bf[0], emb_bf[1], where) / num_rows
    first_row = (core * 4 + key1 * 2 + key2) * BLK
    diag_mask = lax.broadcasted_iota(jnp.int32, corr_blk.shape, 0) + first_row == lax.broadcasted_iota(jnp.int32, corr_blk.shape, 1)
    loss_part = jnp.sum(jnp.where(diag_mask, (1.0 - corr_blk) ** 2, lam_off * (corr_blk * corr_blk)))
    grad_blk = jnp.where(diag_mask, -2.0 * (1.0 - corr_blk), 2.0 * lam_off * corr_blk).astype(jnp.bfloat16)
    grad_corr = gather_blocks(grad_blk, where)
    grad_emb_a = lax.dot_general(emb_bf[1], grad_corr, (((1,), (1,)), ((), ())), preferred_element_type=jnp.float32)
    grad_emb_b = jnp.dot(emb_bf[0], grad_corr, preferred_element_type=jnp.float32)
    grad_emb = jnp.stack([grad_emb_a, grad_emb_b]) / num_rows
    local_sums = jnp.stack([jnp.sum(grad_emb, axis=1), jnp.sum(grad_emb * emb_norm, axis=1)]).reshape(4, -1)
    loss_row = jnp.full((1, local_sums.shape[1]), loss_part, jnp.float32)
    totals = sum_devices(jnp.concatenate([local_sums, loss_row, jnp.zeros((3, local_sums.shape[1]), jnp.float32)]), 3)
    total_loss = totals[4, 0]
    totals = totals[:4].reshape(2, 2, -1) / num_rows
    grad_proj = (inv_three * (grad_emb - totals[0][:, None, :] - emb_norm * totals[1][:, None, :])).astype(jnp.bfloat16)
    flat = lambda t: t.reshape(-1, t.shape[-1])
    third_blk = weight_grad(flat(hid_two), flat(grad_proj), where)
    grad_hid_two = jnp.einsum('wof,ef->woe', grad_proj, w_third, preferred_element_type=jnp.float32)
    grad_pre_two, grad_gain_second, grad_shift_second = affine_backward(grad_hid_two, post_two, norm_two, inv_two, gain_second, num_rows, 4)
    second_blk = weight_grad(flat(hid_one), flat(grad_pre_two), where)
    grad_hid_one = jnp.einsum('wof,ef->woe', grad_pre_two, w_second, preferred_element_type=jnp.float32)
    grad_pre_one, grad_gain_first, grad_shift_first = affine_backward(grad_hid_one, post_one, norm_one, inv_one, gain_first, num_rows, 5)
    first_blk = weight_grad(flat(both_views), flat(grad_pre_one), where)
    grad_third = gather_blocks(third_blk, where)
    grad_second = gather_blocks(second_blk, where)
    grad_first = gather_blocks(first_blk, where)
    return (total_loss, grad_first, grad_second, grad_third, grad_gain_first, grad_shift_first, grad_gain_second, grad_shift_second)


def solution(mesh):
    row_spec = P(ROW_AXES, None)
    repl_spec = P()
    return jax.shard_map(device_step, mesh=mesh, in_specs=(row_spec, row_spec) + (repl_spec,) * 8, out_specs=(repl_spec,) * 8, check_vma=False)
```

time: 1290 us -> 981 us (0.76)
  waiting for transfers between devices: 726 us -> 392 us
  blocking collectives: 143 us -> 0 us
  other arithmetic: 64.6 us -> 141 us
  Pallas kernels: 0 us -> 62.3 us
  starting transfers between devices: 0.08 us -> 36.2 us
  between operations: 18.5 us -> 2.26 us
    psum x2 -> x0, waiting for transfers between devices: 726 us -> none  [the longest x1 519 us: device_step(): lax.psum(jnp.einsum('vnf,vnd->fd', both_views, grad_pre_one, preferred_el...]
    ppermute x0 -> x44, waiting for transfers between devices: none -> 392 us  [send(): return lax.ppermute(block, ROW_AXES, perm)]
    psum x6 -> x0, blocking collectives: 143 us -> none  [the longest x3 73 us: batch_norm(): totals = lax.psum(local_sums, ROW_AXES) / num_rows]
    pallas_call x0 -> x6, Pallas kernels: none -> 62.3 us  [sum_devices(): pl.pallas_call(exchange_kernel, out_shape=jax.ShapeDtypeStruct(vals.shape...]
    dynamic_update_slice x0 -> x28, local copies, waits for them, and re-layouts: none -> 44.8 us  [the longest x16 24.1 us: gather_blocks(): lax.dynamic_update_slice_in_dim(out, far, ((1 - core) * 4 + oidx) * BLK,...]
    ppermute x0 -> x44, starting transfers between devices: none -> 36.2 us  [send(): return lax.ppermute(block, ROW_AXES, perm)]
    gather x1 -> x0, local copies, waits for them, and re-layouts: 33.8 us -> none  [loss_and_grad(): on_diag = jnp.diagonal(corr_mat)]
    add x0 -> x9, other arithmetic: none -> 31.5 us  [the longest x4 16.5 us: reduce_block(): in_k = send(block_of(ours, b_sk) + block_of(got, b_sk), FIRST_PERM)]
  transfers between devices with their start and end apart: 2 -> 44, of which waited for: 2 -> 20; matrix products, arithmetic and copies ran while one was open for 4% -> 25% of each run, Pallas kernels for 0% -> 3%
where the time goes in v1:
time: 981 us; the launch traced here: 972 us
  waiting for transfers between devices  392 us (40%)
  matrix products  258 us (26%)
  other arithmetic  141 us (14%)
  local copies, waits for them, and re-layouts  80.1 us (8%)
  Pallas kernels  62.3 us (6%)
  starting transfers between devices  36.2 us (4%)
    ppermute x44, waiting for transfers between devices, send(): return lax.ppermute(block, ROW_AXES, perm)  392 us
    dot_general x8, matrix products, dot_rows(): lax.dot_general(lhs, rhs, (((0,), (0,)), ((), ())), preferred_element_typ...  101 us
    pallas_call x6, Pallas kernels, sum_devices(): pl.pallas_call(exchange_kernel, out_shape=jax.ShapeDtypeStruct(vals.shape...  62.3 us
    dot_general x2, matrix products, run_layer(): jnp.einsum('vnf,fd->vnd', hidden, weight, preferred_element_type=jnp.floa...  45 us
    ppermute x44, starting transfers between devices, send(): return lax.ppermute(block, ROW_AXES, perm)  36.2 us
    dot_general x1, matrix products, device_step(): jnp.einsum('wof,ef->woe', grad_proj, w_third, preferred_element_type=jnp....  28.9 us
    dot_general x1, matrix products, device_step(): jnp.einsum('wof,ef->woe', grad_pre_two, w_second, preferred_element_type=...  28.9 us
    convert_element_type x2, other arithmetic, affine_backward(): grad_pre.astype(jnp.bfloat16)  27.4 us
  transfers between devices with their start and end apart: 44, of which 20 were waited for; matrix products, arithmetic and copies ran while one was open for 25% of the time, Pallas kernels for 3%

profile of v1, /device:TPU:0, one launch (start us, length us, event | category | flops | bytes accessed | tf_op | source)
XLA Modules:
  0.0 972.4 jit_solution(11475217261581180883)
XLA Ops:
  0.7 24.2 %fusion.54 = (f32[2,2048]{1,0:T(2,128)S(1)}, f32[2,2048]{1,0:T(2,128)S(1)}, f32[2,1024,2048]{2,1,0:T(8,128)}) fusion(bf16[2048,2048]{1,0:T(8,128)(2,1)} %param.12, bf16[1,1024,2048]{2,1,0:T(8,128)(2,1)} %bitcast.95, bf16[1,1024,2048]{2,1,0:T(8,128)(2,1)} %bitcast.97), kind=kOutput, calls=%fused_computation.147 | convolution fusion | flops 17196638208 | bytes 33587200 | tf_op jit(solution)/shard_map/vnf,fd->vnd/dot_general | solution.py:123
  25.6 9.8 %stat_sum.6 = f32[4,2048]{1,0:T(4,128)} custom-call(f32[4,2048]{1,0:T(4,128)} %reshape.185.in_ref), custom_call_target="tpu_custom_call" | custom-call | tf_op jit(solution)/shard_map/stat_sum/pallas_call | solution.py:42
  37.4 7.6 maximum_convert_fusion.1
  45.7 20.8 %fusion.53 = (f32[2,2048]{1,0:T(2,128)S(1)}, f32[2,2048]{1,0:T(2,128)S(1)}, f32[2,1024,2048]{2,1,0:T(8,128)}) fusion(bf16[2,1024,2048]{2,1,0:T(8,128)(2,1)S(1)} %maximum_convert_fusion.1, bf16[2048,2048]{1,0:T(8,128)(2,1)S(1)} %copy-done.24), kind=kOutput, calls=%fused_computation.146 | convolution fusion | flops 17192443904 | bytes 33587200 | tf_op jit(solution)/shard_map/vnf,fd->vnd/dot_general | solution.py:123
  67.1 7.9 stat_sum.7
  76.5 7.5 maximum_convert_fusion
  84.0 24.2 %fusion.52 = (f32[2,2048]{1,0:T(2,128)S(1)}, f32[2,2048]{1,0:T(2,128)S(1)}, f32[2,1024,2048]{2,1,0:T(8,128)}) fusion(bf16[2,1024,2048]{2,1,0:T(8,128)(2,1)S(1)} %maximum_convert_fusion, bf16[2048,2048]{1,0:T(8,128)(2,1)} %param.14), kind=kOutput, calls=%fused_computation.145 | convolution fusion | flops 17192443904 | bytes 33587200 | tf_op jit(solution)/shard_map/vnf,fd->vnd/dot_general | solution.py:144
  108.9 7.9 stat_sum.8
  117.6 7.2 fusion
  130.4 10.6 %fusion.29 = f32[1024,2048]{1,0:T(8,128)} fusion(bf16[2,1024,2048]{2,1,0:T(8,128)(2,1)} %copy-done.1, bf16[1,1024,2048]{2,1,0:T(8,128)(2,1)} %slice.95, s32[]{:T(128)S(6)} %select_n.58), kind=kOutput, calls=%fused_computation.48 | convolution fusion | flops 4294967296 | bytes 14680068 | tf_op jit(solution)/shard_map/dot_general | solution.py:102
  141.2 7.5 fusion.30
  160.5 24.0 %collective-permute-done.2 = f32[256,2048]{1,0:T(8,128)} collective-permute-done((f32[256,2048]{1,0:T(8,128)}, f32[256,2048]{1,0:T(8,128)}, u32[]{:S(2)}, u32[]{:S(2)}) %collective-permute-start.2) | collective-permute-done | bytes 2097184 | tf_op jit(solution)/shard_map/ppermute | solution.py:59
  191.3 31.3 %collective-permute-done.1 = f32[256,2048]{1,0:T(8,128)} collective-permute-done((f32[256,2048]{1,0:T(8,128)S(1)}, f32[256,2048]{1,0:T(8,128)}, u32[]{:S(2)}, u32[]{:S(2)}) %collective-permute-start.1) | collective-permute-done | bytes 2097184 | tf_op jit(solution)/shard_map/ppermute | solution.py:59
  222.6 6.1 collective-permute-done.3
  243.1 22.1 %collective-permute-done.5 = bf16[256,2048]{1,0:T(8,128)(2,1)} collective-permute-done((bf16[256,2048]{1,0:T(8,128)(2,1)}, bf16[256,2048]{1,0:T(8,128)(2,1)}, u32[]{:S(2)}, u32[]{:S(2)}) %collective-permute-start.5) | collective-permute-done | bytes 1048608 | tf_op jit(solution)/shard_map/ppermute | solution.py:59
  267.9 6.2 pad_maximum_fusion
  290.4 12.7 %convolution_bitcast_fusion.1 = f32[1,1024,2048]{2,1,0:T(8,128)S(1)} fusion(bf16[2048,2048]{1,0:T(8,128)(2,1)} %constant_dynamic-update-slice_fusion.23, bf16[2,1024,2048]{2,1,0:T(8,128)(2,1)} %copy-done.1), kind=kOutput, calls=%fused_computation.33 | convolution fusion | flops 8589934592 | bytes 20971520 | tf_op jit(solution)/shard_map/dot_general | solution.py:153
  303.1 17.8 %convolution_bitcast_fusion = f32[1,1024,2048]{2,1,0:T(8,128)} fusion(bf16[2048,2048]{1,0:T(8,128)(2,1)} %constant_dynamic-update-slice_fusion.23, bf16[2,1024,2048]{2,1,0:T(8,128)(2,1)} %copy-done.1), kind=kOutput, calls=%fused_computation.32 | convolution fusion | flops 8589934592 | bytes 20971520 | tf_op jit(solution)/shard_map/dot_general | solution.py:154
  320.9 6.6 fusion.1
  328.3 10.8 %stat_sum.9 = f32[8,2048]{1,0:T(8,128)} custom-call(f32[8,2048]{1,0:T(8,128)} %maximum_maximum_fusion.in_ref), custom_call_target="tpu_custom_call" | custom-call | tf_op jit(solution)/shard_map/stat_sum/pallas_call | solution.py:42
  339.9 15.4 %multiply_convert_fusion.2 = bf16[2,1024,2048]{2,1,0:T(8,128)(2,1)} fusion(f32[2,1024,2048]{2,1,0:T(8,128)} %get-tuple-element.58, f32[1,1024,2048]{2,1,0:T(8,128)} %convolution_bitcast_fusion, f32[1,1024,2048]{2,1,0:T(8,128)} %copy-done, f32[2,2048]{1,0:T(2,128)S(1)} %get-tuple-element.53, f32[2,2048]{1,0:T(2,128)S(1)} %get-tuple-element.52, ...), kind=kLoop, calls=%fused_computation.5 | loop fusion | flops 37748736 | bytes 42008576 | tf_op jit(solution)/shard_map/convert_element_type | solution.py:161
  355.3 28.9 %multiply_reduce_fusion.1 = (f32[2,2048]{1,0:T(2,128)S(1)}, f32[2,2048]{1,0:T(2,128)S(1)}, f32[2,1024,2048]{2,1,0:T(8,128)}) fusion(f32[2,1024,2048]{2,1,0:T(8,128)} %get-tuple-element.57, f32[2,2048]{1,0:T(2,128)S(1)} %get-tuple-element.50, f32[2,2048]{1,0:T(2,128)S(1)} %get-tuple-element.51, bf16[2,1024,2048]{2,1,0:T(8,128)(2,1)} %multiply_convert_fusion.2, ...), kind=kOutput, calls=%fused_computation.4 | convolution fusion | flops 17217609728 | bytes 50413568 | tf_op jit(solution)/shard_map/wof,ef->woe/dot_general | solution.py:164
  384.1 14.9 %fusion.17 = f32[1024,2048]{1,0:T(8,128)} fusion(bf16[2048,2048]{1,0:T(8,128)(2,1)} %bitcast.81, bf16[2048,2048]{1,0:T(8,128)(2,1)} %bitcast.91, s32[]{:T(128)S(6)} %select_n.58), kind=kOutput, calls=%fused_computation.36 | convolution fusion | flops 8589934592 | bytes 20971524 | tf_op jit(solution)/shard_map/dot_general | solution.py:102
  400.4 13.0 %stat_sum.10 = f32[4,2048]{1,0:T(4,128)} custom-call(f32[4,2048]{1,0:T(4,128)} %reshape.190.in_ref), custom_call_target="tpu_custom_call" | custom-call | tf_op jit(solution)/shard_map/stat_sum/pallas_call | solution.py:42
  414.9 15.3 %multiply_convert_fusion.1 = bf16[2,1024,2048]{2,1,0:T(8,128)(2,1)} fusion(f32[2,1024,2048]{2,1,0:T(8,128)} %get-tuple-element.59, f32[2,1024,2048]{2,1,0:T(8,128)} %get-tuple-element.57, f32[2,2048]{1,0:T(2,128)S(1)} %get-tuple-element.42, f32[2,2048]{1,0:T(2,128)S(1)} %get-tuple-element.43, f32[2,2048]{1,0:T(2,128)S(1)} %copy-done.17, ...), kind=kLoop, calls=%fused_computation.3 | loop fusion | flops 29360128 | bytes 42024960 | tf_op jit(solution)/shard_map/convert_element_type | solution.py:134
  430.1 28.9 %multiply_reduce_fusion = (f32[2,2048]{1,0:T(2,128)S(1)}, f32[2,2048]{1,0:T(2,128)S(1)}, f32[2,1024,2048]{2,1,0:T(8,128)}) fusion(f32[2,1024,2048]{2,1,0:T(8,128)} %get-tuple-element.56, f32[2,2048]{1,0:T(2,128)S(1)} %copy-done.13, f32[2,2048]{1,0:T(2,128)S(1)} %copy-done.15, bf16[2,1024,2048]{2,1,0:T(8,128)(2,1)} %multiply_convert_fusion.1, ...), kind=kOutput, calls=%fused_computation.2 | convolution fusion | flops 17217609728 | bytes 50413568 | tf_op jit(solution)/shard_map/wof,ef->woe/dot_general | solution.py:167
  459.0 15.1 %fusion.21 = f32[1024,2048]{1,0:T(8,128)} fusion(bf16[2048,2048]{1,0:T(8,128)(2,1)} %bitcast.83, bf16[2048,2048]{1,0:T(8,128)(2,1)} %bitcast.89, s32[]{:T(128)S(6)} %select_n.58), kind=kOutput, calls=%fused_computation.40 | convolution fusion | flops 8589934592 | bytes 20971524 | tf_op jit(solution)/shard_map/dot_general | solution.py:102
  475.2 13.0 %stat_sum.11 = f32[4,2048]{1,0:T(4,128)} custom-call(f32[4,2048]{1,0:T(4,128)} %reshape.191.in_ref), custom_call_target="tpu_custom_call" | custom-call | tf_op jit(solution)/shard_map/stat_sum/pallas_call | solution.py:42
  489.7 12.1 %multiply_convert_fusion = bf16[2,1024,2048]{2,1,0:T(8,128)(2,1)S(1)} fusion(f32[2,1024,2048]{2,1,0:T(8,128)} %get-tuple-element.60, f32[2,1024,2048]{2,1,0:T(8,128)} %get-tuple-element.56, f32[2,2048]{1,0:T(2,128)S(1)} %get-tuple-element.44, f32[2,2048]{1,0:T(2,128)S(1)} %get-tuple-element.45, f32[2,2048]{1,0:T(2,128)S(1)} %copy-done.16, ...), kind=kLoop, calls=%fused_computation.1 | loop fusion | flops 29360128 | bytes 42024960 | tf_op jit(solution)/shard_map/convert_element_type | solution.py:134
  501.8 13.4 %fusion.25 = f32[1024,2048]{1,0:T(8,128)} fusion(bf16[2048,2048]{1,0:T(8,128)(2,1)S(1)} %bitcast.87, bf16[2048,2048]{1,0:T(8,128)(2,1)} %bitcast.93, s32[]{:T(128)S(6)} %select_n.58), kind=kOutput, calls=%fused_computation.44 | convolution fusion | flops 8589934592 | bytes 20971524 | tf_op jit(solution)/shard_map/dot_general | solution.py:102
  515.6 15.0 %fusion.19 = f32[1024,2048]{1,0:T(8,128)} fusion(bf16[2048,2048]{1,0:T(8,128)(2,1)} %bitcast.82, bf16[2048,2048]{1,0:T(8,128)(2,1)} %bitcast.92, s32[]{:T(128)S(6)} %select_n.56), kind=kOutput, calls=%fused_computation.38 | convolution fusion | flops 8589934592 | bytes 20971524 | tf_op jit(solution)/shard_map/dot_general | solution.py:102
  530.7 13.2 %fusion.23 = f32[1024,2048]{1,0:T(8,128)} fusion(bf16[2048,2048]{1,0:T(8,128)(2,1)S(1)} %bitcast.86, bf16[2048,2048]{1,0:T(8,128)(2,1)} %bitcast.90, s32[]{:T(128)S(6)} %select_n.56), kind=kOutput, calls=%fused_computation.42 | convolution fusion | flops 8589934592 | bytes 20971524 | tf_op jit(solution)/shard_map/dot_general | solution.py:102
  543.8 6.8 dynamic-slice_add_fusion.1
  556.9 11.2 %fusion.27 = f32[1024,2048]{1,0:T(8,128)S(1)} fusion(bf16[2048,2048]{1,0:T(8,128)(2,1)S(1)} %bitcast.88, bf16[2048,2048]{1,0:T(8,128)(2,1)} %bitcast.94, s32[]{:T(128)S(6)} %select_n.56), kind=kOutput, calls=%fused_computation.46 | convolution fusion | flops 8589934592 | bytes 20971524 | tf_op jit(solution)/shard_map/dot_general | solution.py:102
  583.2 32.9 %collective-permute-done.24 = f32[256,2048]{1,0:T(8,128)} collective-permute-done((f32[256,2048]{1,0:T(8,128)S(1)}, f32[256,2048]{1,0:T(8,128)}, u32[]{:S(2)}, u32[]{:S(2)}) %collective-permute-start.24) | collective-permute-done | bytes 2097184 | tf_op jit(solution)/shard_map/ppermute | solution.py:59
  622.9 21.1 %collective-permute-done.13 = f32[256,2048]{1,0:T(8,128)S(1)} collective-permute-done((f32[256,2048]{1,0:T(8,128)S(1)}, f32[256,2048]{1,0:T(8,128)S(1)}, u32[]{:S(2)}, u32[]{:S(2)}) %collective-permute-start.13) | collective-permute-done | bytes 2097184 | tf_op jit(solution)/shard_map/ppermute | solution.py:59
  647.1 40.0 %collective-permute-done.34 = f32[256,2048]{1,0:T(8,128)S(1)} collective-permute-done((f32[256,2048]{1,0:T(8,128)}, f32[256,2048]{1,0:T(8,128)S(1)}, u32[]{:S(2)}, u32[]{:S(2)}) %collective-permute-start.34) | collective-permute-done | bytes 2097184 | tf_op jit(solution)/shard_map/ppermute | solution.py:59
  696.5 35.6 %collective-permute-done.23 = f32[256,2048]{1,0:T(8,128)} collective-permute-done((f32[256,2048]{1,0:T(8,128)}, f32[256,2048]{1,0:T(8,128)}, u32[]{:S(2)}, u32[]{:S(2)}) %collective-permute-start.23) | collective-permute-done | bytes 2097184 | tf_op jit(solution)/shard_map/ppermute | solution.py:59
  735.3 8.3 broadcast.94.clone.1
  743.6 6.7 constant_dynamic-update-slice_fusion.8
  750.2 26.8 %collective-permute-done.12 = f32[256,2048]{1,0:T(8,128)S(1)} collective-permute-done((f32[256,2048]{1,0:T(8,128)S(1)}, f32[256,2048]{1,0:T(8,128)S(1)}, u32[]{:S(2)}, u32[]{:S(2)}) %collective-permute-start.12) | collective-permute-done | bytes 2097184 | tf_op jit(solution)/shard_map/ppermute | solution.py:59
  786.2 35.8 %collective-permute-done.40 = f32[256,2048]{1,0:T(8,128)} collective-permute-done((f32[256,2048]{1,0:T(8,128)}, f32[256,2048]{1,0:T(8,128)}, u32[]{:S(2)}, u32[]{:S(2)}) %collective-permute-start.40) | collective-permute-done | bytes 2097184 | tf_op jit(solution)/shard_map/ppermute | solution.py:59
  827.4 39.5 %collective-permute-done.29 = f32[256,2048]{1,0:T(8,128)} collective-permute-done((f32[256,2048]{1,0:T(8,128)}, f32[256,2048]{1,0:T(8,128)}, u32[]{:S(2)}, u32[]{:S(2)}) %collective-permute-start.29) | collective-permute-done | bytes 2097184 | tf_op jit(solution)/shard_map/ppermute | solution.py:59
  878.6 12.6 %collective-permute-done.18 = f32[256,2048]{1,0:T(8,128)S(1)} collective-permute-done((f32[256,2048]{1,0:T(8,128)S(1)}, f32[256,2048]{1,0:T(8,128)S(1)}, u32[]{:S(2)}, u32[]{:S(2)}) %collective-permute-start.18) | collective-permute-done | bytes 2097184 | tf_op jit(solution)/shard_map/ppermute | solution.py:59
  900.0 13.6 %collective-permute-done.42 = f32[256,2048]{1,0:T(8,128)S(1)} collective-permute-done((f32[256,2048]{1,0:T(8,128)}, f32[256,2048]{1,0:T(8,128)S(1)}, u32[]{:S(2)}, u32[]{:S(2)}) %collective-permute-start.42) | collective-permute-done | bytes 2097184 | tf_op jit(solution)/shard_map/ppermute | solution.py:59
  923.2 13.0 %collective-permute-done.31 = f32[256,2048]{1,0:T(8,128)S(1)} collective-permute-done((f32[256,2048]{1,0:T(8,128)}, f32[256,2048]{1,0:T(8,128)S(1)}, u32[]{:S(2)}, u32[]{:S(2)}) %collective-permute-start.31) | collective-permute-done | bytes 2097184 | tf_op jit(solution)/shard_map/ppermute | solution.py:59
  939.3 19.3 %collective-permute-done.20 = f32[256,2048]{1,0:T(8,128)S(1)} collective-permute-done((f32[256,2048]{1,0:T(8,128)S(1)}, f32[256,2048]{1,0:T(8,128)S(1)}, u32[]{:S(2)}, u32[]{:S(2)}) %collective-permute-start.20) | collective-permute-done | bytes 2097184 | tf_op jit(solution)/shard_map/ppermute | solution.py:59
  965.8 6.2 copy-done.2
  (207 shorter events, 169.8 us)
Async XLA Ops:
  0.6 36.7 %copy-start.22 = (f32[2048]{0:T(1024)S(1)}, f32[2048]{0:T(1024)}, u32[]{:S(2)}) copy-start(f32[2048]{0:T(1024)} %param.16) | copy-start | bytes 24580
  141.1 13.1 %collective-permute-start = (f32[1024,2048]{1,0:T(8,128)}, f32[1024,2048]{1,0:T(8,128)}, u32[]{:S(2)}, u32[]{:S(2)}) collective-permute-start(f32[1024,2048]{1,0:T(8,128)} %fusion.29), channel_id=1, source_target_pairs={{0,1},{1,0},{2,3},{3,2},{4,5},{5,4},{6,7},{7,6}} | collective-permute-start | bytes 25165832 | tf_op jit(solution)/shard_map/ppermute | solution.py:59
  158.5 26.0 %collective-permute-start.2 = (f32[256,2048]{1,0:T(8,128)}, f32[256,2048]{1,0:T(8,128)}, u32[]{:S(2)}, u32[]{:S(2)}) collective-permute-start(f32[256,2048]{1,0:T(8,128)} %get-tuple-element.41), channel_id=1, source_target_pairs={{0,2},{1,5},{2,0},{3,7},{4,6},{5,1},{6,4},{7,3}} | collective-permute-start | bytes 6291464 | tf_op jit(solution)/shard_map/ppermute | solution.py:59
  160.0 62.6 %collective-permute-start.1 = (f32[256,2048]{1,0:T(8,128)S(1)}, f32[256,2048]{1,0:T(8,128)}, u32[]{:S(2)}, u32[]{:S(2)}) collective-permute-start(f32[256,2048]{1,0:T(8,128)S(1)} %get-tuple-element.40), channel_id=1, source_target_pairs={{0,2},{1,5},{2,0},{3,7},{4,6},{5,1},{6,4},{7,3}} | collective-permute-start | bytes 6291464 | tf_op jit(solution)/shard_map/ppermute | solution.py:59
  189.4 39.3 %collective-permute-start.3 = (f32[256,2048]{1,0:T(8,128)}, f32[256,2048]{1,0:T(8,128)}, u32[]{:S(2)}, u32[]{:S(2)}) collective-permute-start(f32[256,2048]{1,0:T(8,128)} %add_add_fusion.6), channel_id=1, source_target_pairs={{0,4},{1,3},{2,6},{3,1},{4,0},{5,7},{6,2},{7,5}} | collective-permute-start | bytes 6291464 | tf_op jit(solution)/shard_map/ppermute | solution.py:59
  240.1 25.2 %collective-permute-start.5 = (bf16[256,2048]{1,0:T(8,128)(2,1)}, bf16[256,2048]{1,0:T(8,128)(2,1)}, u32[]{:S(2)}, u32[]{:S(2)}) collective-permute-start(bf16[256,2048]{1,0:T(8,128)(2,1)} %get-tuple-element.33), channel_id=1, source_target_pairs={{0,4},{1,3},{2,6},{3,1},{4,0},{5,7},{6,2},{7,5}} | collective-permute-start | bytes 3145736 | tf_op jit(solution)/shard_map/ppermute | solution.py:59
  241.4 26.1 %collective-permute-start.7 = (bf16[256,2048]{1,0:T(8,128)(2,1)}, bf16[256,2048]{1,0:T(8,128)(2,1)S(1)}, u32[]{:S(2)}, u32[]{:S(2)}) collective-permute-start(bf16[256,2048]{1,0:T(8,128)(2,1)} %get-tuple-element.33), channel_id=1, source_target_pairs={{0,2},{1,5},{2,0},{3,7},{4,6},{5,1},{6,4},{7,3}} | collective-permute-start | bytes 3145736 | tf_op jit(solution)/shard_map/ppermute | solution.py:59
  243.1 31.9 %collective-permute-start.4 = (bf16[256,2048]{1,0:T(8,128)(2,1)}, bf16[256,2048]{1,0:T(8,128)(2,1)}, u32[]{:S(2)}, u32[]{:S(2)}) collective-permute-start(bf16[256,2048]{1,0:T(8,128)(2,1)} %get-tuple-element.33), channel_id=1, source_target_pairs={{0,1},{1,0},{2,3},{3,2},{4,5},{5,4},{6,7},{7,6}} | collective-permute-start | bytes 3145736 | tf_op jit(solution)/shard_map/ppermute | solution.py:59
  265.2 15.0 %collective-permute-start.9 = (bf16[256,2048]{1,0:T(8,128)(2,1)}, bf16[256,2048]{1,0:T(8,128)(2,1)S(1)}, u32[]{:S(2)}, u32[]{:S(2)}) collective-permute-start(bf16[256,2048]{1,0:T(8,128)(2,1)} %collective-permute-done.5), channel_id=1, source_target_pairs={{0,2},{1,5},{2,0},{3,7},{4,6},{5,1},{6,4},{7,3}} | collective-permute-start | bytes 3145736 | tf_op jit(solution)/shard_map/ppermute | solution.py:59
  267.4 15.1 %collective-permute-start.6 = (bf16[256,2048]{1,0:T(8,128)(2,1)}, bf16[256,2048]{1,0:T(8,128)(2,1)}, u32[]{:S(2)}, u32[]{:S(2)}) collective-permute-start(bf16[256,2048]{1,0:T(8,128)(2,1)} %collective-permute-done.5), channel_id=1, source_target_pairs={{0,1},{1,0},{2,3},{3,2},{4,5},{5,4},{6,7},{7,6}} | collective-permute-start | bytes 3145736 | tf_op jit(solution)/shard_map/ppermute | solution.py:59
  267.4 18.5 %collective-permute-start.8 = (bf16[256,2048]{1,0:T(8,128)(2,1)S(1)}, bf16[256,2048]{1,0:T(8,128)(2,1)}, u32[]{:S(2)}, u32[]{:S(2)}) collective-permute-start(bf16[256,2048]{1,0:T(8,128)(2,1)S(1)} %collective-permute-done.7), channel_id=1, source_target_pairs={{0,1},{1,0},{2,3},{3,2},{4,5},{5,4},{6,7},{7,6}} | collective-permute-start | bytes 3145736 | tf_op jit(solution)/shard_map/ppermute | solution.py:59
  280.2 9.1 collective-permute-start.10
  399.0 144.8 %collective-permute-start.33 = (f32[1024,2048]{1,0:T(8,128)}, f32[1024,2048]{1,0:T(8,128)}, u32[]{:S(2)}, u32[]{:S(2)}) collective-permute-start(f32[1024,2048]{1,0:T(8,128)} %fusion.17), channel_id=1, source_target_pairs={{0,1},{1,0},{2,3},{3,2},{4,5},{5,4},{6,7},{7,6}} | collective-permute-start | bytes 25165832 | tf_op jit(solution)/shard_map/ppermute | solution.py:59
  474.1 78.3 %collective-permute-start.22 = (f32[1024,2048]{1,0:T(8,128)}, f32[1024,2048]{1,0:T(8,128)}, u32[]{:S(2)}, u32[]{:S(2)}) collective-permute-start(f32[1024,2048]{1,0:T(8,128)} %fusion.21), channel_id=1, source_target_pairs={{0,1},{1,0},{2,3},{3,2},{4,5},{5,4},{6,7},{7,6}} | collective-permute-start | bytes 25165832 | tf_op jit(solution)/shard_map/ppermute | solution.py:59
  515.2 52.9 %collective-permute-start.11 = (f32[1024,2048]{1,0:T(8,128)}, f32[1024,2048]{1,0:T(8,128)S(1)}, u32[]{:S(2)}, u32[]{:S(2)}) collective-permute-start(f32[1024,2048]{1,0:T(8,128)} %fusion.25), channel_id=1, source_target_pairs={{0,1},{1,0},{2,3},{3,2},{4,5},{5,4},{6,7},{7,6}} | collective-permute-start | bytes 25165832 | tf_op jit(solution)/shard_map/ppermute | solution.py:59
  550.6 26.0 %collective-permute-start.35 = (f32[256,2048]{1,0:T(8,128)}, f32[256,2048]{1,0:T(8,128)}, u32[]{:S(2)}, u32[]{:S(2)}) collective-permute-start(f32[256,2048]{1,0:T(8,128)} %get-tuple-element.35), channel_id=1, source_target_pairs={{0,2},{1,5},{2,0},{3,7},{4,6},{5,1},{6,4},{7,3}} | collective-permute-start | bytes 6291464 | tf_op jit(solution)/shard_map/ppermute | solution.py:59
  556.7 59.4 %collective-permute-start.24 = (f32[256,2048]{1,0:T(8,128)S(1)}, f32[256,2048]{1,0:T(8,128)}, u32[]{:S(2)}, u32[]{:S(2)}) collective-permute-start(f32[256,2048]{1,0:T(8,128)S(1)} %get-tuple-element.37), channel_id=1, source_target_pairs={{0,2},{1,5},{2,0},{3,7},{4,6},{5,1},{6,4},{7,3}} | collective-permute-start | bytes 6291464 | tf_op jit(solution)/shard_map/ppermute | solution.py:59
  568.2 77.1 %copy-start.5 = (f32[1024,2048]{1,0:T(8,128)}, f32[1024,2048]{1,0:T(8,128)S(1)}, u32[]{:S(2)}) copy-start(f32[1024,2048]{1,0:T(8,128)S(1)} %fusion.27) | copy-start | bytes 25165828
  568.2 77.1 %copy-start.4 = (f32[1024,2048]{1,0:T(8,128)}, f32[1024,2048]{1,0:T(8,128)S(1)}, u32[]{:S(2)}) copy-start(f32[1024,2048]{1,0:T(8,128)S(1)} %collective-permute-done.11) | copy-start | bytes 25165828
  569.3 74.7 %collective-permute-start.13 = (f32[256,2048]{1,0:T(8,128)S(1)}, f32[256,2048]{1,0:T(8,128)S(1)}, u32[]{:S(2)}, u32[]{:S(2)}) collective-permute-start(f32[256,2048]{1,0:T(8,128)S(1)} %get-tuple-element.39), channel_id=1, source_target_pairs={{0,2},{1,5},{2,0},{3,7},{4,6},{5,1},{6,4},{7,3}} | collective-permute-start | bytes 6291464 | tf_op jit(solution)/shard_map/ppermute | solution.py:59
  571.1 116.0 %collective-permute-start.34 = (f32[256,2048]{1,0:T(8,128)}, f32[256,2048]{1,0:T(8,128)S(1)}, u32[]{:S(2)}, u32[]{:S(2)}) collective-permute-start(f32[256,2048]{1,0:T(8,128)} %get-tuple-element.34), channel_id=1, source_target_pairs={{0,2},{1,5},{2,0},{3,7},{4,6},{5,1},{6,4},{7,3}} | collective-permute-start | bytes 6291464 | tf_op jit(solution)/shard_map/ppermute | solution.py:59
  580.1 108.4 %collective-permute-start.36 = (f32[256,2048]{1,0:T(8,128)S(1)}, f32[256,2048]{1,0:T(8,128)}, u32[]{:S(2)}, u32[]{:S(2)}) collective-permute-start(f32[256,2048]{1,0:T(8,128)S(1)} %add_add_fusion), channel_id=1, source_target_pairs={{0,4},{1,3},{2,6},{3,1},{4,0},{5,7},{6,2},{7,5}} | collective-permute-start | bytes 6291464 | tf_op jit(solution)/shard_map/ppermute | solution.py:59
  581.3 150.8 %collective-permute-start.23 = (f32[256,2048]{1,0:T(8,128)}, f32[256,2048]{1,0:T(8,128)}, u32[]{:S(2)}, u32[]{:S(2)}) collective-permute-start(f32[256,2048]{1,0:T(8,128)} %get-tuple-element.36), channel_id=1, source_target_pairs={{0,2},{1,5},{2,0},{3,7},{4,6},{5,1},{6,4},{7,3}} | collective-permute-start | bytes 6291464 | tf_op jit(solution)/shard_map/ppermute | solution.py:59
  616.1 160.9 %collective-permute-start.12 = (f32[256,2048]{1,0:T(8,128)S(1)}, f32[256,2048]{1,0:T(8,128)S(1)}, u32[]{:S(2)}, u32[]{:S(2)}) collective-permute-start(f32[256,2048]{1,0:T(8,128)S(1)} %get-tuple-element.38), channel_id=1, source_target_pairs={{0,2},{1,5},{2,0},{3,7},{4,6},{5,1},{6,4},{7,3}} | collective-permute-start | bytes 6291464 | tf_op jit(solution)/shard_map/ppermute | solution.py:59
  644.0 89.2 %collective-permute-start.25 = (f32[256,2048]{1,0:T(8,128)}, f32[256,2048]{1,0:T(8,128)}, u32[]{:S(2)}, u32[]{:S(2)}) collective-permute-start(f32[256,2048]{1,0:T(8,128)} %add_add_fusion.2), channel_id=1, source_target_pairs={{0,4},{1,3},{2,6},{3,1},{4,0},{5,7},{6,2},{7,5}} | collective-permute-start | bytes 6291464 | tf_op jit(solution)/shard_map/ppermute | solution.py:59
  687.1 89.9 %collective-permute-start.14 = (f32[256,2048]{1,0:T(8,128)}, f32[256,2048]{1,0:T(8,128)}, u32[]{:S(2)}, u32[]{:S(2)}) collective-permute-start(f32[256,2048]{1,0:T(8,128)} %add_add_fusion.4), channel_id=1, source_target_pairs={{0,4},{1,3},{2,6},{3,1},{4,0},{5,7},{6,2},{7,5}} | collective-permute-start | bytes 6291464 | tf_op jit(solution)/shard_map/ppermute | solution.py:59
  696.5 81.7 %copy-start.3 = (f32[2048,2048]{1,0:T(8,128)}, f32[2048,2048]{1,0:T(8,128)S(1)}, u32[]{:S(2)}) copy-start(f32[2048,2048]{1,0:T(8,128)S(1)} %get-tuple-element.24) | copy-start | bytes 50331652
  696.5 81.7 %collective-permute-start.37 = (f32[256,2048]{1,0:T(8,128)}, f32[256,2048]{1,0:T(8,128)}, u32[]{:S(2)}, u32[]{:S(2)}) collective-permute-start(f32[256,2048]{1,0:T(8,128)} %get-tuple-element.25), channel_id=1, source_target_pairs={{0,1},{1,0},{2,3},{3,2},{4,5},{5,4},{6,7},{7,6}} | collective-permute-start | bytes 6291464 | tf_op jit(solution)/shard_map/ppermute | solution.py:59
  732.1 54.1 %collective-permute-start.38 = (f32[256,2048]{1,0:T(8,128)}, f32[256,2048]{1,0:T(8,128)}, u32[]{:S(2)}, u32[]{:S(2)}) collective-permute-start(f32[256,2048]{1,0:T(8,128)} %get-tuple-element.25), channel_id=1, source_target_pairs={{0,4},{1,3},{2,6},{3,1},{4,0},{5,7},{6,2},{7,5}} | collective-permute-start | bytes 6291464 | tf_op jit(solution)/shard_map/ppermute | solution.py:59
  733.2 88.7 %collective-permute-start.40 = (f32[256,2048]{1,0:T(8,128)}, f32[256,2048]{1,0:T(8,128)}, u32[]{:S(2)}, u32[]{:S(2)}) collective-permute-start(f32[256,2048]{1,0:T(8,128)} %get-tuple-element.25), channel_id=1, source_target_pairs={{0,2},{1,5},{2,0},{3,7},{4,6},{5,1},{6,4},{7,3}} | collective-permute-start | bytes 6291464 | tf_op jit(solution)/shard_map/ppermute | solution.py:59
  777.0 46.1 %collective-permute-start.26 = (f32[256,2048]{1,0:T(8,128)}, f32[256,2048]{1,0:T(8,128)}, u32[]{:S(2)}, u32[]{:S(2)}) collective-permute-start(f32[256,2048]{1,0:T(8,128)} %get-tuple-element.27), channel_id=1, source_target_pairs={{0,1},{1,0},{2,3},{3,2},{4,5},{5,4},{6,7},{7,6}} | collective-permute-start | bytes 6291464 | tf_op jit(solution)/shard_map/ppermute | solution.py:59
  777.0 50.3 %collective-permute-start.27 = (f32[256,2048]{1,0:T(8,128)}, f32[256,2048]{1,0:T(8,128)}, u32[]{:S(2)}, u32[]{:S(2)}) collective-permute-start(f32[256,2048]{1,0:T(8,128)} %get-tuple-element.27), channel_id=1, source_target_pairs={{0,4},{1,3},{2,6},{3,1},{4,0},{5,7},{6,2},{7,5}} | collective-permute-start | bytes 6291464 | tf_op jit(solution)/shard_map/ppermute | solution.py:59
  778.2 88.7 %collective-permute-start.29 = (f32[256,2048]{1,0:T(8,128)}, f32[256,2048]{1,0:T(8,128)}, u32[]{:S(2)}, u32[]{:S(2)}) collective-permute-start(f32[256,2048]{1,0:T(8,128)} %get-tuple-element.27), channel_id=1, source_target_pairs={{0,2},{1,5},{2,0},{3,7},{4,6},{5,1},{6,4},{7,3}} | collective-permute-start | bytes 6291464 | tf_op jit(solution)/shard_map/ppermute | solution.py:59
  786.2 80.7 %collective-permute-start.15 = (f32[256,2048]{1,0:T(8,128)S(1)}, f32[256,2048]{1,0:T(8,128)S(1)}, u32[]{:S(2)}, u32[]{:S(2)}) collective-permute-start(f32[256,2048]{1,0:T(8,128)S(1)} %get-tuple-element.29), channel_id=1, source_target_pairs={{0,1},{1,0},{2,3},{3,2},{4,5},{5,4},{6,7},{7,6}} | collective-permute-start | bytes 6291464 | tf_op jit(solution)/shard_map/ppermute | solution.py:59
  822.0 50.3 %collective-permute-start.16 = (f32[256,2048]{1,0:T(8,128)S(1)}, f32[256,2048]{1,0:T(8,128)S(1)}, u32[]{:S(2)}, u32[]{:S(2)}) collective-permute-start(f32[256,2048]{1,0:T(8,128)S(1)} %get-tuple-element.29), channel_id=1, source_target_pairs={{0,4},{1,3},{2,6},{3,1},{4,0},{5,7},{6,2},{7,5}} | collective-permute-start | bytes 6291464 | tf_op jit(solution)/shard_map/ppermute | solution.py:59
  823.1 68.1 %collective-permute-start.18 = (f32[256,2048]{1,0:T(8,128)S(1)}, f32[256,2048]{1,0:T(8,128)S(1)}, u32[]{:S(2)}, u32[]{:S(2)}) collective-permute-start(f32[256,2048]{1,0:T(8,128)S(1)} %get-tuple-element.29), channel_id=1, source_target_pairs={{0,2},{1,5},{2,0},{3,7},{4,6},{5,1},{6,4},{7,3}} | collective-permute-start | bytes 6291464 | tf_op jit(solution)/shard_map/ppermute | solution.py:59
  827.3 67.0 %collective-permute-start.39 = (f32[256,2048]{1,0:T(8,128)}, f32[256,2048]{1,0:T(8,128)S(1)}, u32[]{:S(2)}, u32[]{:S(2)}) collective-permute-start(f32[256,2048]{1,0:T(8,128)} %collective-permute-done.38), channel_id=1, source_target_pairs={{0,1},{1,0},{2,3},{3,2},{4,5},{5,4},{6,7},{7,6}} | collective-permute-start | bytes 6291464 | tf_op jit(solution)/shard_map/ppermute | solution.py:59
  866.9 32.4 %collective-permute-start.41 = (f32[256,2048]{1,0:T(8,128)}, f32[256,2048]{1,0:T(8,128)S(1)}, u32[]{:S(2)}, u32[]{:S(2)}) collective-permute-start(f32[256,2048]{1,0:T(8,128)} %collective-permute-done.40), channel_id=1, source_target_pairs={{0,1},{1,0},{2,3},{3,2},{4,5},{5,4},{6,7},{7,6}} | collective-permute-start | bytes 6291464 | tf_op jit(solution)/shard_map/ppermute | solution.py:59
  866.9 46.8 %collective-permute-start.42 = (f32[256,2048]{1,0:T(8,128)}, f32[256,2048]{1,0:T(8,128)S(1)}, u32[]{:S(2)}, u32[]{:S(2)}) collective-permute-start(f32[256,2048]{1,0:T(8,128)} %collective-permute-done.38), channel_id=1, source_target_pairs={{0,2},{1,5},{2,0},{3,7},{4,6},{5,1},{6,4},{7,3}} | collective-permute-start | bytes 6291464 | tf_op jit(solution)/shard_map/ppermute | solution.py:59
  872.3 46.0 %collective-permute-start.28 = (f32[256,2048]{1,0:T(8,128)}, f32[256,2048]{1,0:T(8,128)S(1)}, u32[]{:S(2)}, u32[]{:S(2)}) collective-permute-start(f32[256,2048]{1,0:T(8,128)} %collective-permute-done.27), channel_id=1, source_target_pairs={{0,1},{1,0},{2,3},{3,2},{4,5},{5,4},{6,7},{7,6}} | collective-permute-start | bytes 6291464 | tf_op jit(solution)/shard_map/ppermute | solution.py:59
  891.2 30.5 %collective-permute-start.30 = (f32[256,2048]{1,0:T(8,128)}, f32[256,2048]{1,0:T(8,128)S(1)}, u32[]{:S(2)}, u32[]{:S(2)}) collective-permute-start(f32[256,2048]{1,0:T(8,128)} %collective-permute-done.29), channel_id=1, source_target_pairs={{0,1},{1,0},{2,3},{3,2},{4,5},{5,4},{6,7},{7,6}} | collective-permute-start | bytes 6291464 | tf_op jit(solution)/shard_map/ppermute | solution.py:59
  894.3 41.8 %collective-permute-start.31 = (f32[256,2048]{1,0:T(8,128)}, f32[256,2048]{1,0:T(8,128)S(1)}, u32[]{:S(2)}, u32[]{:S(2)}) collective-permute-start(f32[256,2048]{1,0:T(8,128)} %collective-permute-done.27), channel_id=1, source_target_pairs={{0,2},{1,5},{2,0},{3,7},{4,6},{5,1},{6,4},{7,3}} | collective-permute-start | bytes 6291464 | tf_op jit(solution)/shard_map/ppermute | solution.py:59
  899.3 59.3 %collective-permute-start.20 = (f32[256,2048]{1,0:T(8,128)S(1)}, f32[256,2048]{1,0:T(8,128)S(1)}, u32[]{:S(2)}, u32[]{:S(2)}) collective-permute-start(f32[256,2048]{1,0:T(8,128)S(1)} %collective-permute-done.16), channel_id=1, source_target_pairs={{0,2},{1,5},{2,0},{3,7},{4,6},{5,1},{6,4},{7,3}} | collective-permute-start | bytes 6291464 | tf_op jit(solution)/shard_map/ppermute | solution.py:59
  913.7 47.9 %collective-permute-start.17 = (f32[256,2048]{1,0:T(8,128)S(1)}, f32[256,2048]{1,0:T(8,128)S(1)}, u32[]{:S(2)}, u32[]{:S(2)}) collective-permute-start(f32[256,2048]{1,0:T(8,128)S(1)} %collective-permute-done.16), channel_id=1, source_target_pairs={{0,1},{1,0},{2,3},{3,2},{4,5},{5,4},{6,7},{7,6}} | collective-permute-start | bytes 6291464 | tf_op jit(solution)/shard_map/ppermute | solution.py:59
  918.3 43.8 %collective-permute-start.19 = (f32[256,2048]{1,0:T(8,128)S(1)}, f32[256,2048]{1,0:T(8,128)S(1)}, u32[]{:S(2)}, u32[]{:S(2)}) collective-permute-start(f32[256,2048]{1,0:T(8,128)S(1)} %collective-permute-done.18), channel_id=1, source_target_pairs={{0,1},{1,0},{2,3},{3,2},{4,5},{5,4},{6,7},{7,6}} | collective-permute-start | bytes 6291464 | tf_op jit(solution)/shard_map/ppermute | solution.py:59
  921.7 40.9 %collective-permute-start.43 = (f32[256,2048]{1,0:T(8,128)S(1)}, f32[256,2048]{1,0:T(8,128)S(1)}, u32[]{:S(2)}, u32[]{:S(2)}) collective-permute-start(f32[256,2048]{1,0:T(8,128)S(1)} %collective-permute-done.42), channel_id=1, source_target_pairs={{0,1},{1,0},{2,3},{3,2},{4,5},{5,4},{6,7},{7,6}} | collective-permute-start | bytes 6291464 | tf_op jit(solution)/shard_map/ppermute | solution.py:59
  936.1 28.0 %collective-permute-start.32 = (f32[256,2048]{1,0:T(8,128)S(1)}, f32[256,2048]{1,0:T(8,128)S(1)}, u32[]{:S(2)}, u32[]{:S(2)}) collective-permute-start(f32[256,2048]{1,0:T(8,128)S(1)} %collective-permute-done.31), channel_id=1, source_target_pairs={{0,1},{1,0},{2,3},{3,2},{4,5},{5,4},{6,7},{7,6}} | collective-permute-start | bytes 6291464 | tf_op jit(solution)/shard_map/ppermute | solution.py:59
  958.6 7.0 collective-permute-start.21
  (27 other events, 491.0 us)
